TPU v7x, 32 devices: a whole 2x2x4 slice. The times are simulated.
32 devices in a mesh: dp: 2 (over core), tensor: 16 (over z, y, x).
Axes of the slice: x: 2, y: 2, z: 4, core: 2. Of those that a mesh axis runs over, the one named last changes fastest.
Arguments:
- gradient: float32 [2, 8192, 512], P('dp', 'tensor'), may hold values from -80 to 80
Outputs:
- update: bfloat16 [2, 8192, 512], P(None, 'tensor')
All inputs are finite; a program needn't handle non-finite values.
Results may differ from a plain program's by a relative error of at most 0.001.
Values may be sent and summed in bfloat16 or wider, within the bound.
No kernel may reach another device: no remote copies, remote signals or barrier semaphores. Data moves between devices by JAX's collectives and lax.ppermute only.
A program may use at most 64 MiB of HBM per device.

v0:
```python
import math
import jax
import jax.numpy as jnp
from jax import lax
from jax.sharding import PartitionSpec as P

FEATURES = 8192
OUTPUTS = 512
ITERS = 3
linear_term = 3.4445
cubic_term = -4.775
quintic_term = 2.0315
norm_floor = 1e-07
update_gain = 0.2


def multiply(first_factor, second_factor):
    return jnp.einsum("mrs,mst->mrt", first_factor, second_factor, precision=lax.Precision.HIGHEST)


def local_gram(gradient):
    return jnp.einsum("mfr,mfs->mrs", gradient, gradient, precision=lax.Precision.HIGHEST)


def reduce_gram(partial_gram):
    return lax.psum(partial_gram, "tensor")


def replicated_total(gram_matrix):
    order = gram_matrix.shape[2]
    identity = jnp.eye(order, dtype=jnp.float32)[None]
    running = identity
    for turn_index in range(ITERS):
        squared = multiply(gram_matrix, gram_matrix)
        polynomial = linear_term * identity + cubic_term * gram_matrix + quintic_term * squared
        if turn_index == 0:
            running = polynomial
        else:
            running = multiply(running, polynomial)
        if turn_index + 1 < ITERS:
            gram_matrix = multiply(multiply(polynomial, gram_matrix), polynomial)
    return running


def on_device(gradient):
    summed = reduce_gram(local_gram(gradient))
    squared_norm = jnp.trace(summed, axis1=1, axis2=2)
    divisor = jnp.sqrt(squared_norm) + norm_floor
    gram_matrix = summed / (divisor * divisor)[:, None, None]
    polished = jnp.einsum(
        "mfr,mrs->mfs", gradient, replicated_total(gram_matrix), precision=lax.Precision.HIGHEST
    )
    factor = update_gain * math.sqrt(max(FEATURES, OUTPUTS)) / divisor
    update = (factor[:, None, None] * polished).astype(jnp.bfloat16)
    return lax.all_gather(update, "dp", axis=0, tiled=True)


def solution(mesh):
    placed = (P("dp", "tensor", None),)
    return jax.shard_map(
        on_device, mesh=mesh, in_specs=placed, out_specs=P(None, "tensor", None), check_vma=False
    )
```

profile of v0, /device:TPU:0, one launch (start us, length us, event | category | flops | bytes accessed | tf_op | source)
XLA Modules:
  0.0 171.5 jit_solution(2133667007509548431)
XLA Ops:
  6.5 0.0 copy-start
  6.5 0.0 all-reduce.2.cloned.1.call-start
  6.5 1.2 copy-done
  7.8 2.8 %convolution_bitcast_fusion = f32[1,512,512]{2,1,0:T(8,128)} fusion(f32[1,512,512]{2,1,0:T(8,128)S(1)} %copy-done), kind=kOutput, calls=%fused_computation.9 | convolution fusion | flops 1610612736 | bytes 2097152 | tf_op jit(solution)/shard_map/mfr,mfs->mrs/dot_general | solution.py:22
  10.6 0.0 all-reduce.2.cloned.1.call-update
  10.6 0.0 all-gather.3.cloned.1.call-start
  10.7 117.1 %all-reduce.2.cloned.1.call-done = f32[1,512,512]{2,1,0:T(8,128)} async-done(((f32[1,512,512]{2,1,0:T(8,128)}), f32[1,512,512]{2,1,0:T(8,128)}) %all-reduce.2.cloned.1.call-update) | async-done | bytes 1048592 | tf_op jit(solution)/shard_map/psum | solution.py:26
  127.8 0.0 copy-start.1
  127.8 2.0 %select_reduce_fusion = f32[]{:T(128)} fusion(f32[1,512,512]{2,1,0:T(8,128)} %all-reduce.2.cloned.1.call-done), kind=kLoop, calls=%fused_computation.20 | loop fusion | flops 786431 | bytes 1048580 | tf_op jit(solution)/shard_map/jit(trace)/reduce_sum | solution.py:47
  130.5 0.0 copy-done.1
  130.5 1.9 %fusion.4 = f32[512,512]{1,0:T(8,128)S(1)} fusion(f32[1,512,512]{2,1,0:T(8,128)S(1)} %copy-done.1, f32[]{:T(128)S(6)} %mul.52), kind=kOutput, calls=%fused_computation.11 | convolution fusion | flops 1612709888 | bytes 2097156 | tf_op jit(solution)/shard_map/mrs,mst->mrt/dot_general | solution.py:18
  132.5 1.9 %fusion.7 = f32[512,512]{1,0:T(8,128)S(1)} fusion(f32[512,512]{1,0:T(8,128)S(1)} %fusion.4, f32[1,512,512]{2,1,0:T(8,128)S(1)} %copy-done.1, f32[]{:T(128)S(6)} %mul.52), kind=kOutput, calls=%fused_computation.14 | convolution fusion | flops 1610874880 | bytes 3145732 | tf_op jit(solution)/shard_map/mrs,mst->mrt/dot_general | solution.py:18
  134.3 1.8 %fusion.12 = f32[512,512]{1,0:T(8,128)S(1)} fusion(f32[512,512]{1,0:T(8,128)S(1)} %fusion.7, f32[512,512]{1,0:T(8,128)S(1)} %fusion.4), kind=kOutput, calls=%fused_computation.23 | convolution fusion | flops 1610612736 | bytes 3145728 | tf_op jit(solution)/shard_map/mrs,mst->mrt/dot_general | solution.py:18
  136.2 1.9 %fusion.1 = f32[512,512]{1,0:T(8,128)S(1)} fusion(f32[512,512]{1,0:T(8,128)S(1)} %fusion.12), kind=kOutput, calls=%fused_computation.6 | convolution fusion | flops 1612185600 | bytes 2097152 | tf_op jit(solution)/shard_map/mrs,mst->mrt/dot_general | solution.py:18
  138.1 2.8 %fusion.14 = f32[512,512]{1,0:T(8,128)} fusion(f32[512,512]{1,0:T(8,128)S(1)} %fusion.1, f32[512,512]{1,0:T(8,128)S(1)} %fusion.12), kind=kOutput, calls=%fused_computation.25 | convolution fusion | flops 1610612736 | bytes 3145728 | tf_op jit(solution)/shard_map/mrs,mst->mrt/dot_general | solution.py:18
  140.9 1.8 %fusion.13 = f32[512,512]{1,0:T(8,128)S(1)} fusion(f32[512,512]{1,0:T(8,128)S(1)} %fusion.4, f32[512,512]{1,0:T(8,128)S(1)} %fusion.1), kind=kOutput, calls=%fused_computation.24 | convolution fusion | flops 1610612736 | bytes 3145728 | tf_op jit(solution)/shard_map/mrs,mst->mrt/dot_general | solution.py:18
  142.8 3.2 %fusion.15 = f32[512,512]{1,0:T(8,128)S(1)} fusion(f32[512,512]{1,0:T(8,128)} %fusion.14, f32[512,512]{1,0:T(8,128)S(1)} %fusion.1), kind=kOutput, calls=%fused_computation.26 | convolution fusion | flops 1610612736 | bytes 3145728 | tf_op jit(solution)/shard_map/mrs,mst->mrt/dot_general | solution.py:18
  146.1 1.9 %fusion = f32[512,512]{1,0:T(8,128)S(1)} fusion(f32[512,512]{1,0:T(8,128)S(1)} %fusion.15), kind=kOutput, calls=%fused_computation.4 | convolution fusion | flops 1612185600 | bytes 2097152 | tf_op jit(solution)/shard_map/mrs,mst->mrt/dot_general | solution.py:18
  148.0 1.8 %fusion.16 = f32[512,512]{1,0:T(8,128)S(1)} fusion(f32[512,512]{1,0:T(8,128)S(1)} %fusion.13, f32[512,512]{1,0:T(8,128)S(1)} %fusion), kind=kOutput, calls=%fused_computation.27 | convolution fusion | flops 1610612736 | bytes 3145728 | tf_op jit(solution)/shard_map/mrs,mst->mrt/dot_general | solution.py:18
  149.8 4.3 %fusion.6 = bf16[512,512]{0,1:T(8,128)(2,1)} fusion(f32[512,512]{1,0:T(8,128)S(1)} %fusion.16, f32[1,512,512]{2,1,0:T(8,128)S(1)} %copy-done, f32[]{:T(128)S(6)} %div.12), kind=kOutput, calls=%fused_computation.13 | convolution fusion | flops 1611137024 | bytes 2621444 | tf_op jit(solution)/shard_map/mfr,mrs->mfs/dot_general | solution.py:50
  154.1 0.0 all-gather.3.cloned.1.call-update
  154.1 8.3 %all-gather.3.cloned.1.call-done = bf16[1024,512]{0,1:T(8,128)(2,1)} async-done(((bf16[512,512]{0,1:T(8,128)(2,1)}), bf16[1024,512]{0,1:T(8,128)(2,1)}) %all-gather.3.cloned.1.call-update) | async-done | bytes 1048592 | tf_op jit(solution)/shard_map/all_gather | solution.py:55
  162.4 2.3 %copy.3 = bf16[1024,512]{1,0:T(8,128)(2,1)} copy(bf16[1024,512]{0,1:T(8,128)(2,1)} %all-gather.3.cloned.1.call-done) | data formatting | bytes 2097152 | tf_op jit(solution)/shard_map/all_gather | solution.py:55
Async XLA Ops:
  6.5 1.2 copy-start
  6.5 121.3 %all-reduce.2.cloned.1.call-start = ((), (), s32[]{:S(2)}) async-start(), calls=%async_computation | async-start | bytes 2097152 | tf_op jit(solution)/shard_map/psum | solution.py:26
  10.6 151.8 %all-gather.3.cloned.1.call-start = ((), (), s32[]{:S(2)}) async-start(), calls=%async_computation.1 | async-start | bytes 1572864 | tf_op jit(solution)/shard_map/all_gather | solution.py:55
  127.8 2.7 %copy-start.1 = (f32[1,512,512]{2,1,0:T(8,128)S(1)}, f32[1,512,512]{2,1,0:T(8,128)}, u32[]{:S(2)}) copy-start(f32[1,512,512]{2,1,0:T(8,128)} %all-reduce.2.cloned.1.call-done) | copy-start | bytes 3145732
Sparse Core Ops, SparseCore 0:
  12.6 115.1 all-reduce.1
  154.2 8.0 all-gather.2
where the time goes:
time: 172 us; the launch traced here: 171 us
  waiting for transfers between devices  125 us (73%)
  matrix products  26.3 us (15%)
  between operations  14.2 us (8%)
  local copies, waits for them, and re-layouts  3.5 us (2%)
  other arithmetic  1.99 us (1%)
    psum x1, waiting for transfers between devices, reduce_gram(): return lax.psum(partial_gram, 'tensor')  117 us
    dot_general x9, matrix products, multiply(): jnp.einsum('mrs,mst->mrt', first_factor, second_factor, precision=lax.Pre...  19.2 us
    all_gather x1, waiting for transfers between devices, on_device(): return lax.all_gather(update, 'dp', axis=0, tiled=True)  8.26 us
    dot_general x1, matrix products, on_device(): jnp.einsum('mfr,mrs->mfs', gradient, replicated_total(gram_matrix), preci...  4.28 us
  transfers between devices with their start and end apart: 2, of which 2 were waited for; matrix products, arithmetic and copies ran while one was open for 0% of the time, Pallas kernels for 0%

commit v1 on v0

--- a/solution.py
+++ b/solution.py
@@ -23,7 +23,7 @@
 
 
 def reduce_gram(partial_gram):
-    return lax.psum(partial_gram, "tensor")
+    return jnp.sum(lax.all_gather(partial_gram, "tensor"), axis=0)
 
 
 def replicated_total(gram_matrix):

time: 172 us -> 254 us (1.48)
  waiting for transfers between devices: 125 us -> 201 us
  other arithmetic: 1.99 us -> 8.58 us
    all_gather x0 -> x1, waiting for transfers between devices: none -> 194 us  [reduce_gram(): return jnp.sum(lax.all_gather(partial_gram, 'tensor'), axis=0)]
    psum x1 -> x0, waiting for transfers between devices: 117 us -> none  [reduce_gram(): return lax.psum(partial_gram, 'tensor')]
    reduce_sum x0 -> x1, other arithmetic: none -> 7.91 us  [reduce_gram(): return jnp.sum(lax.all_gather(partial_gram, 'tensor'), axis=0)]
where the time goes in v1:
time: 254 us
  waiting for transfers between devices  201 us (79%)
  matrix products  26.3 us (10%)
  between operations  14.2 us (6%)
  other arithmetic  8.58 us (3%)
  local copies, waits for them, and re-layouts  3.5 us (1%)
    all_gather x1, waiting for transfers between devices, reduce_gram(): return jnp.sum(lax.all_gather(partial_gram, 'tensor'), axis=0)  194 us
    dot_general x9, matrix products, multiply(): jnp.einsum('mrs,mst->mrt', first_factor, second_factor, precision=lax.Pre...  19.2 us
    reduce_sum x1, other arithmetic, reduce_gram(): return jnp.sum(lax.all_gather(partial_gram, 'tensor'), axis=0)  7.91 us
    all_gather x1, waiting for transfers between devices, on_device(): return lax.all_gather(update, 'dp', axis=0, tiled=True)  7.37 us
  transfers between devices with their start and end apart: 2, of which 2 were waited for; matrix products, arithmetic and copies ran while one was open for 0% of the time, Pallas kernels for 0%

profile of v1, /device:TPU:0, one launch (start us, length us, event | category | flops | bytes accessed | tf_op | source)
XLA Modules:
  0.0 253.9 jit_solution(12230029904456417315)
XLA Ops:
  6.5 0.0 copy-start
  6.5 0.0 all-gather.5.cloned.1.call-start
  6.5 1.2 copy-done
  7.8 2.8 %fusion.6 = f32[512,512]{1,0:T(8,128)} fusion(f32[1,512,512]{2,1,0:T(8,128)S(1)} %copy-done), kind=kOutput, calls=%fused_computation.13 | convolution fusion | flops 1610612736 | bytes 2097152 | tf_op jit(solution)/shard_map/mfr,mfs->mrs/dot_general | solution.py:22
  10.6 0.0 all-gather.5.cloned.1.call-update
  10.6 0.0 all-gather.7.cloned.1.call-start
  10.7 193.8 %all-gather.5.cloned.1.call-done = f32[8192,512]{1,0:T(8,128)} async-done(((f32[512,512]{1,0:T(8,128)}), f32[8192,512]{1,0:T(8,128)}) %all-gather.5.cloned.1.call-update) | async-done | bytes 16777232 | tf_op jit(solution)/shard_map/all_gather | solution.py:26
  204.5 7.9 %reduce.2 = f32[512,512]{1,0:T(8,128)S(1)} reduce(f32[16,512,512]{2,1,0:T(8,128)} %bitcast.25, f32[]{:T(128)} %constant.7.clone.1), dimensions={0}, to_apply=%region_0.0 | reduce | flops 3932160 | bytes 17825796 | tf_op jit(solution)/shard_map/reduce_sum | solution.py:26
  212.4 0.7 select_reduce_fusion
  213.8 1.9 fusion.2
  215.7 1.9 fusion.8
  217.6 1.8 fusion.9
  219.5 1.9 fusion.1
  221.4 2.8 %fusion.11 = f32[512,512]{1,0:T(8,128)} fusion(f32[512,512]{1,0:T(8,128)S(1)} %fusion.1, f32[512,512]{1,0:T(8,128)S(1)} %fusion.9), kind=kOutput, calls=%fused_computation.21 | convolution fusion | flops 1610612736 | bytes 3145728 | tf_op jit(solution)/shard_map/mrs,mst->mrt/dot_general | solution.py:18
  224.2 2.0 fusion.10
  226.3 3.1 %fusion.12 = f32[512,512]{1,0:T(8,128)S(1)} fusion(f32[512,512]{1,0:T(8,128)} %fusion.11, f32[512,512]{1,0:T(8,128)S(1)} %fusion.1), kind=kOutput, calls=%fused_computation.22 | convolution fusion | flops 1610612736 | bytes 3145728 | tf_op jit(solution)/shard_map/mrs,mst->mrt/dot_general | solution.py:18
  229.3 1.9 fusion
  231.2 1.8 fusion.13
  233.1 4.3 %fusion.4 = bf16[512,512]{0,1:T(8,128)(2,1)} fusion(f32[512,512]{1,0:T(8,128)S(1)} %fusion.13, f32[1,512,512]{2,1,0:T(8,128)S(1)} %copy-done, f32[]{:T(128)S(6)} %div.23), kind=kOutput, calls=%fused_computation.11 | convolution fusion | flops 1611137024 | bytes 2621444 | tf_op jit(solution)/shard_map/mfr,mrs->mfs/dot_general | solution.py:50
  237.4 0.0 all-gather.7.cloned.1.call-update
  237.4 7.4 %all-gather.7.cloned.1.call-done = bf16[1024,512]{0,1:T(8,128)(2,1)} async-done(((bf16[512,512]{0,1:T(8,128)(2,1)}), bf16[1024,512]{0,1:T(8,128)(2,1)}) %all-gather.7.cloned.1.call-update) | async-done | bytes 1048592 | tf_op jit(solution)/shard_map/all_gather | solution.py:55
  244.8 2.3 copy.3
Async XLA Ops:
  6.5 1.2 copy-start
  6.5 198.0 %all-gather.5.cloned.1.call-start = ((), (), s32[]{:S(2)}) async-start(), calls=%async_computation | async-start | bytes 17825792 | tf_op jit(solution)/shard_map/all_gather | solution.py:26
  10.6 234.2 %all-gather.7.cloned.1.call-start = ((), (), s32[]{:S(2)}) async-start(), calls=%async_computation.1 | async-start | bytes 1572864 | tf_op jit(solution)/shard_map/all_gather | solution.py:55
Sparse Core Ops, SparseCore 0:
  10.7 193.7 all-gather.4
  237.5 7.2 all-gather.6
